TPU v7x, 16 devices: a whole 2x2x2 slice. The times are simulated.
16 devices in a mesh: row: 2 (over z), col: 8 (over y, x, core).
Axes of the slice: x: 2, y: 2, z: 2, core: 2. Of those that a mesh axis runs over, the one named last changes fastest.
Arguments:
- v_panels: float32 [8192, 8192], P('row', 'col')
- t_factors: float32 [64, 128, 128], P('col')
- z_vecs: float32 [8192, 4096], P(None, ('row', 'col'))
Outputs:
- output: float32 [8192, 4096], P(None, ('row', 'col'))
All inputs are finite; a program needn't handle non-finite values.
Results may differ from a plain program's by a relative error of at most 0.001.
Values sent between devices are 32-bit elements.
A program may use at most 1 GiB of HBM per device.

v0:
```python
import jax
import jax.numpy as jnp
from jax import lax
from jax.sharding import PartitionSpec as P, NamedSharding

FULL_PREC = lax.Precision.HIGHEST
CONTRACT_ROWS = (((0,), (0,)), ((), ()))


def solution(mesh):
    col_dev = mesh.shape["col"]

    def local_apply(v_loc, t_loc, z_loc):
        num_local = t_loc.shape[0]
        block_w = t_loc.shape[1]
        x_two = lax.all_to_all(z_loc, "row", 0, 1, tiled=True)

        def outer_step(step_idx, x_cur):
            local_idx = num_local - 1 - step_idx
            v_own = lax.dynamic_slice_in_dim(v_loc, local_idx * block_w, block_w, axis=1)
            t_own = lax.dynamic_index_in_dim(t_loc, local_idx, axis=0, keepdims=False)
            v_all = lax.all_gather(v_own, "col")
            t_all = lax.all_gather(t_own, "col")

            def inner_step(sub_idx, x_in):
                owner_col = col_dev - 1 - sub_idx
                v_blk = v_all[owner_col]
                t_blk = t_all[owner_col]
                w_part = lax.dot_general(v_blk, x_in, CONTRACT_ROWS, precision=FULL_PREC, preferred_element_type=jnp.float32)
                w_sum = lax.psum(w_part, "row")
                y_blk = jnp.dot(t_blk, w_sum, precision=FULL_PREC, preferred_element_type=jnp.float32)
                return x_in - jnp.dot(v_blk, y_blk, precision=FULL_PREC, preferred_element_type=jnp.float32)

            return lax.fori_loop(0, col_dev, inner_step, x_cur)

        x_two = lax.fori_loop(0, num_local, outer_step, x_two)
        return lax.all_to_all(x_two, "row", 1, 0, tiled=True)

    return jax.shard_map(
        local_apply,
        mesh=mesh,
        in_specs=(P("row", "col"), P("col", None, None), P(None, ("row", "col"))),
        out_specs=P(None, ("row", "col")),
        check_vma=False,
    )
```

profile of v0, /device:TPU:0, one launch (start us, length us, event | category | flops | bytes accessed | tf_op | source)
XLA Modules:
  0.0 3663.1 jit_solution(794784475893953510)
XLA Ops:
  13.5 93.9 %all-to-all-done = f32[2,4096,256]{2,1,0:T(8,128)} async-done(((f32[2,4096,256]{2,1,0:T(8,128)}), f32[2,4096,256]{2,1,0:T(8,128)}, u32[]{:S(2)}, u32[]{:S(2)}) %all-to-all-start) | async-done | bytes 8388640 | tf_op jit(solution)/shard_map/all_to_all | solution.py:16
  125.3 3428.7 %while.46 = (s32[]{:T(128)}, f32[4096,512]{1,0:T(8,128)}, f32[4096,1024]{1,0:T(8,128)}, f32[8,128,128]{2,1,0:T(8,128)}, s32[]{:T(128)}, /*index=5*/s32[]{:T(128)...) while((s32[]{:T(128)}, f32[4096,512]{1,0:T(8,128)}, ...), condition=%wide.region_4.5_spmd, body=%wide.region_0.4_spmd.sunk | while | flops 6545276928 | bytes 93585944 | solution.py:36
  139.2 75.4 %all-gather.5.cloned.1.call-done = f32[32768,128]{1,0:T(8,128)} async-done(((f32[4096,128]{1,0:T(8,128)}), f32[32768,128]{1,0:T(8,128)}) %all-gather.5.cloned.1.call-update) | async-done | bytes 16777232 | tf_op jit(solution)/shard_map/while/body/eval_jaxpr/all_gather | solution.py:22
  214.6 339.4 %while.47 = (s32[]{:T(128)}, f32[4096,512]{1,0:T(8,128)}, f32[8,4096,128]{2,1,0:T(8,128)}, f32[8,128,128]{2,1,0:T(8,128)S(1)}, s32[]{:T(128)}, /*index=5*/s32[]{:T(128)}, s32[]{:T(128)}, s32[]{:T(128)}) while((s32[]{:T(128)}, f32[4096,512]{1,0:T(8,128)}, f32[8,4096,128]{2,1,0:T(8,128)}, f32[8,128,128]{2,1,0:T(8,128)S(1)}, s32[]{:T(128)}, ...), condition=%wide.region_3.3_spmd, body=%wide.region_1.2_spmd.sunk | while | flops 6545276928 | bytes 32047288 | solution.py:34
  224.4 19.5 all-reduce.2.cloned.1.call-done
  266.8 19.5 all-reduce.2.cloned.1.call-done
  309.3 19.4 all-reduce.2.cloned.1.call-done
  351.7 19.4 all-reduce.2.cloned.1.call-done
  394.1 19.4 all-reduce.2.cloned.1.call-done
  436.5 19.4 all-reduce.2.cloned.1.call-done
  479.0 19.4 all-reduce.2.cloned.1.call-done
  567.7 75.4 %all-gather.5.cloned.1.call-done = f32[32768,128]{1,0:T(8,128)} async-done(((f32[4096,128]{1,0:T(8,128)}), f32[32768,128]{1,0:T(8,128)}) %all-gather.5.cloned.1.call-update) | async-done | bytes 16777232 | tf_op jit(solution)/shard_map/while/body/eval_jaxpr/all_gather | solution.py:22
  643.1 339.5 %while.47 = (s32[]{:T(128)}, f32[4096,512]{1,0:T(8,128)}, f32[8,4096,128]{2,1,0:T(8,128)}, f32[8,128,128]{2,1,0:T(8,128)S(1)}, s32[]{:T(128)}, /*index=5*/s32[]{:T(128)}, s32[]{:T(128)}, s32[]{:T(128)}) while((s32[]{:T(128)}, f32[4096,512]{1,0:T(8,128)}, f32[8,4096,128]{2,1,0:T(8,128)}, f32[8,128,128]{2,1,0:T(8,128)S(1)}, s32[]{:T(128)}, ...), condition=%wide.region_3.3_spmd, body=%wide.region_1.2_spmd.sunk | while | flops 6545276928 | bytes 32047288 | solution.py:34
  652.9 19.5 all-reduce.2.cloned.1.call-done
  695.4 19.5 all-reduce.2.cloned.1.call-done
  737.8 19.5 all-reduce.2.cloned.1.call-done
  780.2 19.5 all-reduce.2.cloned.1.call-done
  822.7 19.5 all-reduce.2.cloned.1.call-done
  865.1 19.5 all-reduce.2.cloned.1.call-done
  907.5 19.5 all-reduce.2.cloned.1.call-done
  950.0 19.5 all-reduce.2.cloned.1.call-done
  996.3 75.4 %all-gather.5.cloned.1.call-done = f32[32768,128]{1,0:T(8,128)} async-done(((f32[4096,128]{1,0:T(8,128)}), f32[32768,128]{1,0:T(8,128)}) %all-gather.5.cloned.1.call-update) | async-done | bytes 16777232 | tf_op jit(solution)/shard_map/while/body/eval_jaxpr/all_gather | solution.py:22
  1071.7 339.4 %while.47 = (s32[]{:T(128)}, f32[4096,512]{1,0:T(8,128)}, f32[8,4096,128]{2,1,0:T(8,128)}, f32[8,128,128]{2,1,0:T(8,128)S(1)}, s32[]{:T(128)}, /*index=5*/s32[]{:T(128)}, s32[]{:T(128)}, s32[]{:T(128)}) while((s32[]{:T(128)}, f32[4096,512]{1,0:T(8,128)}, f32[8,4096,128]{2,1,0:T(8,128)}, f32[8,128,128]{2,1,0:T(8,128)S(1)}, s32[]{:T(128)}, ...), condition=%wide.region_3.3_spmd, body=%wide.region_1.2_spmd.sunk | while | flops 6545276928 | bytes 32047288 | solution.py:34
  1081.5 19.5 all-reduce.2.cloned.1.call-done
  1124.0 19.5 all-reduce.2.cloned.1.call-done
  1424.9 75.4 %all-gather.5.cloned.1.call-done = f32[32768,128]{1,0:T(8,128)} async-done(((f32[4096,128]{1,0:T(8,128)}), f32[32768,128]{1,0:T(8,128)}) %all-gather.5.cloned.1.call-update) | async-done | bytes 16777232 | tf_op jit(solution)/shard_map/while/body/eval_jaxpr/all_gather | solution.py:22
  1500.2 339.5 %while.47 = (s32[]{:T(128)}, f32[4096,512]{1,0:T(8,128)}, f32[8,4096,128]{2,1,0:T(8,128)}, f32[8,128,128]{2,1,0:T(8,128)S(1)}, s32[]{:T(128)}, /*index=5*/s32[]{:T(128)}, s32[]{:T(128)}, s32[]{:T(128)}) while((s32[]{:T(128)}, f32[4096,512]{1,0:T(8,128)}, f32[8,4096,128]{2,1,0:T(8,128)}, f32[8,128,128]{2,1,0:T(8,128)S(1)}, s32[]{:T(128)}, ...), condition=%wide.region_3.3_spmd, body=%wide.region_1.2_spmd.sunk | while | flops 6545276928 | bytes 32047288 | solution.py:34
  1510.0 19.5 all-reduce.2.cloned.1.call-done
  1552.5 19.5 all-reduce.2.cloned.1.call-done
  1594.9 19.5 all-reduce.2.cloned.1.call-done
  1637.4 19.5 all-reduce.2.cloned.1.call-done
  1679.8 19.5 all-reduce.2.cloned.1.call-done
  1722.2 19.5 all-reduce.2.cloned.1.call-done
  1764.7 19.5 all-reduce.2.cloned.1.call-done
  1807.1 19.5 all-reduce.2.cloned.1.call-done
  1853.4 75.4 %all-gather.5.cloned.1.call-done = f32[32768,128]{1,0:T(8,128)} async-done(((f32[4096,128]{1,0:T(8,128)}), f32[32768,128]{1,0:T(8,128)}) %all-gather.5.cloned.1.call-update) | async-done | bytes 16777232 | tf_op jit(solution)/shard_map/while/body/eval_jaxpr/all_gather | solution.py:22
  1928.8 339.4 %while.47 = (s32[]{:T(128)}, f32[4096,512]{1,0:T(8,128)}, f32[8,4096,128]{2,1,0:T(8,128)}, f32[8,128,128]{2,1,0:T(8,128)S(1)}, s32[]{:T(128)}, /*index=5*/s32[]{:T(128)}, s32[]{:T(128)}, s32[]{:T(128)}) while((s32[]{:T(128)}, f32[4096,512]{1,0:T(8,128)}, f32[8,4096,128]{2,1,0:T(8,128)}, f32[8,128,128]{2,1,0:T(8,128)S(1)}, s32[]{:T(128)}, ...), condition=%wide.region_3.3_spmd, body=%wide.region_1.2_spmd.sunk | while | flops 6545276928 | bytes 32047288 | solution.py:34
  1938.6 19.5 all-reduce.2.cloned.1.call-done
  1981.1 19.5 all-reduce.2.cloned.1.call-done
  2282.0 75.4 %all-gather.5.cloned.1.call-done = f32[32768,128]{1,0:T(8,128)} async-done(((f32[4096,128]{1,0:T(8,128)}), f32[32768,128]{1,0:T(8,128)}) %all-gather.5.cloned.1.call-update) | async-done | bytes 16777232 | tf_op jit(solution)/shard_map/while/body/eval_jaxpr/all_gather | solution.py:22
  2357.4 339.5 %while.47 = (s32[]{:T(128)}, f32[4096,512]{1,0:T(8,128)}, f32[8,4096,128]{2,1,0:T(8,128)}, f32[8,128,128]{2,1,0:T(8,128)S(1)}, s32[]{:T(128)}, /*index=5*/s32[]{:T(128)}, s32[]{:T(128)}, s32[]{:T(128)}) while((s32[]{:T(128)}, f32[4096,512]{1,0:T(8,128)}, f32[8,4096,128]{2,1,0:T(8,128)}, f32[8,128,128]{2,1,0:T(8,128)S(1)}, s32[]{:T(128)}, ...), condition=%wide.region_3.3_spmd, body=%wide.region_1.2_spmd.sunk | while | flops 6545276928 | bytes 32047288 | solution.py:34
  2367.2 19.5 all-reduce.2.cloned.1.call-done
  2409.6 19.5 all-reduce.2.cloned.1.call-done
  2452.1 19.5 all-reduce.2.cloned.1.call-done
  2494.5 19.5 all-reduce.2.cloned.1.call-done
  2536.9 19.5 all-reduce.2.cloned.1.call-done
  2579.4 19.5 all-reduce.2.cloned.1.call-done
  2621.8 19.5 all-reduce.2.cloned.1.call-done
  2664.2 19.5 all-reduce.2.cloned.1.call-done
  2710.6 75.4 %all-gather.5.cloned.1.call-done = f32[32768,128]{1,0:T(8,128)} async-done(((f32[4096,128]{1,0:T(8,128)}), f32[32768,128]{1,0:T(8,128)}) %all-gather.5.cloned.1.call-update) | async-done | bytes 16777232 | tf_op jit(solution)/shard_map/while/body/eval_jaxpr/all_gather | solution.py:22
  2786.0 339.4 %while.47 = (s32[]{:T(128)}, f32[4096,512]{1,0:T(8,128)}, f32[8,4096,128]{2,1,0:T(8,128)}, f32[8,128,128]{2,1,0:T(8,128)S(1)}, s32[]{:T(128)}, /*index=5*/s32[]{:T(128)}, s32[]{:T(128)}, s32[]{:T(128)}) while((s32[]{:T(128)}, f32[4096,512]{1,0:T(8,128)}, f32[8,4096,128]{2,1,0:T(8,128)}, f32[8,128,128]{2,1,0:T(8,128)S(1)}, s32[]{:T(128)}, ...), condition=%wide.region_3.3_spmd, body=%wide.region_1.2_spmd.sunk | while | flops 6545276928 | bytes 32047288 | solution.py:34
  2795.8 19.5 all-reduce.2.cloned.1.call-done
  2838.2 19.5 all-reduce.2.cloned.1.call-done
  3139.1 75.4 %all-gather.5.cloned.1.call-done = f32[32768,128]{1,0:T(8,128)} async-done(((f32[4096,128]{1,0:T(8,128)}), f32[32768,128]{1,0:T(8,128)}) %all-gather.5.cloned.1.call-update) | async-done | bytes 16777232 | tf_op jit(solution)/shard_map/while/body/eval_jaxpr/all_gather | solution.py:22
  3214.5 339.5 %while.47 = (s32[]{:T(128)}, f32[4096,512]{1,0:T(8,128)}, f32[8,4096,128]{2,1,0:T(8,128)}, f32[8,128,128]{2,1,0:T(8,128)S(1)}, s32[]{:T(128)}, /*index=5*/s32[]{:T(128)}, s32[]{:T(128)}, s32[]{:T(128)}) while((s32[]{:T(128)}, f32[4096,512]{1,0:T(8,128)}, f32[8,4096,128]{2,1,0:T(8,128)}, f32[8,128,128]{2,1,0:T(8,128)S(1)}, s32[]{:T(128)}, ...), condition=%wide.region_3.3_spmd, body=%wide.region_1.2_spmd.sunk | while | flops 6545276928 | bytes 32047288 | solution.py:34
  3224.3 19.5 all-reduce.2.cloned.1.call-done
  3266.7 19.5 all-reduce.2.cloned.1.call-done
  3309.2 19.5 all-reduce.2.cloned.1.call-done
  3351.6 19.5 all-reduce.2.cloned.1.call-done
  3394.0 19.5 all-reduce.2.cloned.1.call-done
  3436.5 19.5 all-reduce.2.cloned.1.call-done
  3478.9 19.5 all-reduce.2.cloned.1.call-done
  3521.3 19.5 all-reduce.2.cloned.1.call-done
  3557.9 95.3 %all_to_all.38 = f32[4096,2,256]{2,0,1:T(8,128)S(1)} all-to-all(f32[4096,2,256]{2,0,1:T(8,128)S(1)} %bitcast.40), channel_id=1, replica_groups=mesh['row'=2,'col'=8] {'row'}, dimensions={1} | all-to-all | bytes 16777216 | tf_op jit(solution)/shard_map/all_to_all | solution.py:37
  (384 shorter events, 1980.7 us)
Async XLA Ops:
  6.5 100.9 %all-to-all-start = ((f32[2,4096,256]{2,1,0:T(8,128)}), f32[2,4096,256]{2,1,0:T(8,128)}, u32[]{:S(2)}, u32[]{:S(2)}) async-start(f32[2,4096,256]{2,1,0:T(8,128)} %bitcast.42), calls=%async_computation | async-start | bytes 16777216 | tf_op jit(solution)/shard_map/all_to_all | solution.py:16
  125.3 89.3 %all-gather.5.cloned.1.call-start = ((), (), s32[]{:S(2)}) async-start(), calls=%async_computation.2 | async-start | bytes 18874368 | tf_op jit(solution)/shard_map/while/body/eval_jaxpr/all_gather | solution.py:22
  214.6 29.3 all-reduce.2.cloned.1.call-start
  257.0 29.3 all-reduce.2.cloned.1.call-start
  299.5 29.3 all-reduce.2.cloned.1.call-start
  384.3 29.3 all-reduce.2.cloned.1.call-start
  426.7 29.3 all-reduce.2.cloned.1.call-start
  469.2 29.3 all-reduce.2.cloned.1.call-start
  511.6 29.3 all-reduce.2.cloned.1.call-start
  554.0 89.1 %all-gather.5.cloned.1.call-start = ((), (), s32[]{:S(2)}) async-start(), calls=%async_computation.2 | async-start | bytes 18874368 | tf_op jit(solution)/shard_map/while/body/eval_jaxpr/all_gather | solution.py:22
  643.1 29.3 all-reduce.2.cloned.1.call-start
  685.6 29.3 all-reduce.2.cloned.1.call-start
  728.0 29.3 all-reduce.2.cloned.1.call-start
  770.4 29.3 all-reduce.2.cloned.1.call-start
  812.9 29.3 all-reduce.2.cloned.1.call-start
  855.3 29.3 all-reduce.2.cloned.1.call-start
  897.7 29.3 all-reduce.2.cloned.1.call-start
  940.2 29.3 all-reduce.2.cloned.1.call-start
  982.6 89.1 %all-gather.5.cloned.1.call-start = ((), (), s32[]{:S(2)}) async-start(), calls=%async_computation.2 | async-start | bytes 18874368 | tf_op jit(solution)/shard_map/while/body/eval_jaxpr/all_gather | solution.py:22
  1071.7 29.3 all-reduce.2.cloned.1.call-start
  1114.2 29.3 all-reduce.2.cloned.1.call-start
  1199.0 29.3 all-reduce.2.cloned.1.call-start
  1241.4 29.3 all-reduce.2.cloned.1.call-start
  1283.9 29.3 all-reduce.2.cloned.1.call-start
  1326.3 29.3 all-reduce.2.cloned.1.call-start
  1368.7 29.3 all-reduce.2.cloned.1.call-start
  1411.1 89.1 %all-gather.5.cloned.1.call-start = ((), (), s32[]{:S(2)}) async-start(), calls=%async_computation.2 | async-start | bytes 18874368 | tf_op jit(solution)/shard_map/while/body/eval_jaxpr/all_gather | solution.py:22
  1500.2 29.3 all-reduce.2.cloned.1.call-start
  1542.7 29.3 all-reduce.2.cloned.1.call-start
  1585.1 29.3 all-reduce.2.cloned.1.call-start
  1627.6 29.3 all-reduce.2.cloned.1.call-start
  1670.0 29.3 all-reduce.2.cloned.1.call-start
  1712.4 29.3 all-reduce.2.cloned.1.call-start
  1754.9 29.3 all-reduce.2.cloned.1.call-start
  1797.3 29.3 all-reduce.2.cloned.1.call-start
  1839.7 89.1 %all-gather.5.cloned.1.call-start = ((), (), s32[]{:S(2)}) async-start(), calls=%async_computation.2 | async-start | bytes 18874368 | tf_op jit(solution)/shard_map/while/body/eval_jaxpr/all_gather | solution.py:22
  1928.8 29.3 all-reduce.2.cloned.1.call-start
  1971.3 29.3 all-reduce.2.cloned.1.call-start
  2056.1 29.3 all-reduce.2.cloned.1.call-start
  2098.6 29.3 all-reduce.2.cloned.1.call-start
  2141.0 29.3 all-reduce.2.cloned.1.call-start
  2183.4 29.3 all-reduce.2.cloned.1.call-start
  2225.8 29.3 all-reduce.2.cloned.1.call-start
  2268.3 89.1 %all-gather.5.cloned.1.call-start = ((), (), s32[]{:S(2)}) async-start(), calls=%async_computation.2 | async-start | bytes 18874368 | tf_op jit(solution)/shard_map/while/body/eval_jaxpr/all_gather | solution.py:22
  2357.4 29.3 all-reduce.2.cloned.1.call-start
  2399.8 29.3 all-reduce.2.cloned.1.call-start
  2442.2 29.3 all-reduce.2.cloned.1.call-start
  2484.7 29.3 all-reduce.2.cloned.1.call-start
  2527.1 29.3 all-reduce.2.cloned.1.call-start
  2569.5 29.3 all-reduce.2.cloned.1.call-start
  2612.0 29.3 all-reduce.2.cloned.1.call-start
  2654.4 29.3 all-reduce.2.cloned.1.call-start
  2696.8 89.1 %all-gather.5.cloned.1.call-start = ((), (), s32[]{:S(2)}) async-start(), calls=%async_computation.2 | async-start | bytes 18874368 | tf_op jit(solution)/shard_map/while/body/eval_jaxpr/all_gather | solution.py:22
  2786.0 29.3 all-reduce.2.cloned.1.call-start
  2828.4 29.3 all-reduce.2.cloned.1.call-start
  3125.4 89.1 %all-gather.5.cloned.1.call-start = ((), (), s32[]{:S(2)}) async-start(), calls=%async_computation.2 | async-start | bytes 18874368 | tf_op jit(solution)/shard_map/while/body/eval_jaxpr/all_gather | solution.py:22
  3214.5 29.3 all-reduce.2.cloned.1.call-start
  3256.9 29.3 all-reduce.2.cloned.1.call-start
  3299.4 29.3 all-reduce.2.cloned.1.call-start
  3341.8 29.3 all-reduce.2.cloned.1.call-start
  3384.2 29.3 all-reduce.2.cloned.1.call-start
  3426.7 29.3 all-reduce.2.cloned.1.call-start
  3469.1 29.3 all-reduce.2.cloned.1.call-start
  3511.5 29.3 all-reduce.2.cloned.1.call-start
  (9 other events, 263.3 us)
Sparse Core Ops, SparseCore 0:
  128.5 86.0 all-gather.4
  224.5 19.3 all-reduce.1
  267.0 19.2 all-reduce.1
  309.4 19.2 all-reduce.1
  351.8 19.2 all-reduce.1
  394.2 19.2 all-reduce.1
  436.7 19.2 all-reduce.1
  479.1 19.2 all-reduce.1
  521.5 19.2 all-reduce.1
  557.2 85.8 all-gather.4
  653.0 19.3 all-reduce.1
  695.5 19.2 all-reduce.1
  737.9 19.2 all-reduce.1
  780.4 19.2 all-reduce.1
  822.8 19.2 all-reduce.1
  865.2 19.2 all-reduce.1
  907.7 19.2 all-reduce.1
  950.1 19.2 all-reduce.1
  985.8 85.8 all-gather.4
  1081.6 19.3 all-reduce.1
  1124.1 19.2 all-reduce.1
  1166.5 19.2 all-reduce.1
  1208.9 19.2 all-reduce.1
  1251.4 19.2 all-reduce.1
  1293.8 19.2 all-reduce.1
  1336.2 19.2 all-reduce.1
  1378.6 19.2 all-reduce.1
  1414.3 85.8 all-gather.4
  1510.2 19.3 all-reduce.1
  1552.6 19.2 all-reduce.1
  1595.0 19.2 all-reduce.1
  1637.5 19.2 all-reduce.1
  1679.9 19.2 all-reduce.1
  1722.3 19.2 all-reduce.1
  1764.8 19.2 all-reduce.1
  1807.2 19.2 all-reduce.1
  1842.9 85.8 all-gather.4
  1938.8 19.3 all-reduce.1
  1981.2 19.2 all-reduce.1
  2023.6 19.2 all-reduce.1
  2066.1 19.2 all-reduce.1
  2108.5 19.2 all-reduce.1
  2150.9 19.2 all-reduce.1
  2271.5 85.8 all-gather.4
  2367.3 19.3 all-reduce.1
  2409.7 19.2 all-reduce.1
  2452.2 19.2 all-reduce.1
  2494.6 19.2 all-reduce.1
  2537.0 19.2 all-reduce.1
  2579.5 19.2 all-reduce.1
  2621.9 19.2 all-reduce.1
  2664.3 19.2 all-reduce.1
  2700.0 85.8 all-gather.4
  2795.9 19.3 all-reduce.1
  2838.3 19.2 all-reduce.1
  3128.6 85.8 all-gather.4
  3224.4 19.3 all-reduce.1
  3266.9 19.2 all-reduce.1
  3309.3 19.2 all-reduce.1
  3351.7 19.2 all-reduce.1
  3394.2 19.2 all-reduce.1
  3436.6 19.2 all-reduce.1
  3479.0 19.2 all-reduce.1
  3521.5 19.2 all-reduce.1
  (8 shorter events, 153.9 us)
where the time goes:
time: 3670 us; the launch traced here: 3660 us
  waiting for transfers between devices  1940 us (53%)
  matrix products  1470 us (40%)
  blocking collectives  174 us (5%)
  local copies, waits for them, and re-layouts  56.4 us (2%)
    psum x64, waiting for transfers between devices, inner_step(): w_sum = lax.psum(w_part, 'row')  1250 us
    dot_general x64, matrix products, inner_step(): jnp.dot(v_blk, y_blk, precision=FULL_PREC, preferred_element_type=jnp.flo...  758 us
    dot_general x64, matrix products, inner_step(): lax.dot_general(v_blk, x_in, CONTRACT_ROWS, precision=FULL_PREC, preferre...  626 us
    all_gather x8, waiting for transfers between devices, outer_step(): v_all = lax.all_gather(v_own, 'col')  603 us
    all_to_all x1, blocking collectives, local_apply(): return lax.all_to_all(x_two, 'row', 1, 0, tiled=True)  95.3 us
    all_to_all x1, waiting for transfers between devices, local_apply(): x_two = lax.all_to_all(z_loc, 'row', 0, 1, tiled=True)  93.9 us
    dot_general x64, matrix products, inner_step(): jnp.dot(t_blk, w_sum, precision=FULL_PREC, preferred_element_type=jnp.flo...  83.9 us
    all_gather x8, blocking collectives, outer_step(): t_all = lax.all_gather(t_own, 'col')  78.5 us
  transfers between devices with their start and end apart: 73, of which 73 were waited for; matrix products, arithmetic and copies ran while one was open for 0% of the time, Pallas kernels for 0%

commit v1 on v0

v1 whole, which is shorter than its diff:
```python
import functools
import jax, jax.numpy as jnp
from jax import lax
from jax.experimental import pallas as pl
from jax.experimental.pallas import tpu as pltpu

BF = jnp.bfloat16
F32 = jnp.float32
TN = (((0,), (0,)), ((), ()))
TR = 512

def split3(v):
    h = v.astype(BF)
    r = v - h.astype(F32)
    m = r.astype(BF)
    l = (r - m.astype(F32)).astype(BF)
    return h, m, l

def mm(a, b):
    return jnp.dot(a, b, preferred_element_type=F32)

def mmt(a, b):
    return lax.dot_general(a, b, TN, preferred_element_type=F32)

def stage1(half, off, p, X, VF, C, XS, YC, upd, wacc, src, dst):
    for r in range(2):
        rows = pl.ds(pl.multiple_of(r * half + off, TR), TR)
        x = X[rows, :]
        if upd:
            x = x - (mm(C[src, 0, rows, :], YC[0]) + mm(C[src, 0, rows, :], YC[1]) + mm(C[src, 1, rows, :], YC[2]))
            X[rows, :] = x
        if wacc:
            prow = pl.ds(r * TR, TR)
            xh, xm, xl = split3(x)
            XS[p, 0, prow, :] = xh
            XS[p, 1, prow, :] = xm
            XS[p, 2, prow, :] = xl
            vh, vm, vl = split3(VF[dst, rows, :])
            C[dst, 0, rows, :128] = vh
            C[dst, 0, rows, 128:] = vm
            C[dst, 1, rows, :128] = vh
            C[dst, 1, rows, 128:] = vl

def stage2(half, off, p, C, XS, A, B, dst):
    a = A[...]
    b = B[...]
    for r in range(2):
        rows = pl.ds(pl.multiple_of(r * half + off, TR), TR)
        prow = pl.ds(r * TR, TR)
        n1 = C[dst, 0, rows, :]
        a += mmt(n1, XS[p, 0, prow, :]) + mmt(n1, XS[p, 1, prow, :])
        b += mmt(C[dst, 1, rows, 128:], XS[p, 0, prow, :]) + mmt(n1[:, :128], XS[p, 2, prow, :])
    A[...] = a
    B[...] = b

def make_y(tq, A, B, YC):
    w = A[:128, :] + A[128:, :] + B[...]
    th, tm, tl = split3(tq)
    wh, wm, wl = split3(w)
    t1 = jnp.concatenate([th, tm], axis=1)
    t2 = jnp.concatenate([th, tl], axis=1)
    y = mm(t1, jnp.concatenate([wh, wh], axis=0)) + mm(t1, jnp.concatenate([wm, wm], axis=0)) + mm(t2, jnp.concatenate([wl, wh], axis=0))
    yh, ym, yl = split3(y)
    YC[0] = jnp.concatenate([yh, yh], axis=0)
    YC[1] = jnp.concatenate([ym, ym], axis=0)
    YC[2] = jnp.concatenate([yl, yh], axis=0)
    A[...] = jnp.zeros_like(A)
    B[...] = jnp.zeros_like(B)

def group_kernel(t, vt, tq, x_in, x_out, X, VF, C, XS, YC, A, B, vsem, xsem):
    half = X.shape[0] // 2
    first = t * TR
    n = half - first
    nt = n // TR
    def xcopy(r, inward):
        sl = pl.ds(r * half + first, n)
        if inward:
            return pltpu.make_async_copy(x_in.at[sl, :], X.at[sl, :], xsem.at[r])
        return pltpu.make_async_copy(X.at[sl, :], x_out.at[sl, :], xsem.at[r])
    def vcopy(q, slot, r):
        return pltpu.make_async_copy(vt.at[r * 8 + q], VF.at[slot, pl.ds(r * half + first, n), :], vsem.at[slot, r])
    for r in range(2):
        xcopy(r, True).start()
        vcopy(7, 1, r).start()
    A[...] = jnp.zeros_like(A)
    B[...] = jnp.zeros_like(B)
    for r in range(2):
        xcopy(r, True).wait()

    def run(upd, wacc, src, dst):
        def s1(i, p):
            stage1(half, first + i * TR, p, X, VF, C, XS, YC, upd, wacc, src, dst)
        def s2(i, p):
            stage2(half, first + i * TR, p, C, XS, A, B, dst)
        if not wacc:
            lax.fori_loop(0, nt, lambda i, c: (s1(i, 0), c)[1], 0)
            return
        s1(0, 0)
        def body(i, c):
            p = lax.rem(i, 2)
            s2(i - 1, 1 - p)
            s1(i, p)
            return c
        lax.fori_loop(1, nt, body, 0)
        s2(nt - 1, (nt - 1) % 2)

    for r in range(2):
        vcopy(6, 0, r).start()
    for r in range(2):
        vcopy(7, 1, r).wait()
    run(False, True, 0, 1)
    make_y(tq[7], A, B, YC)
    def panel(k, c):
        q = 6 - k
        slot = lax.rem(q, 2)
        @pl.when(q > 0)
        def _():
            for r in range(2):
                vcopy(q - 1, 1 - slot, r).start()
        for r in range(2):
            vcopy(q, slot, r).wait()
        run(True, True, 1 - slot, slot)
        make_y(tq[q], A, B, YC)
        return c
    lax.fori_loop(0, 7, panel, 0)
    run(True, False, 0, 1)
    for r in range(2):
        xcopy(r, False).start()
    for r in range(2):
        xcopy(r, False).wait()

def group_call(t, vt, tq, x):
    nrow, ncol = x.shape
    any_spec = pl.BlockSpec(memory_space=pl.ANY)
    flops = 8 * 2 * 2 * 6 * 128 * ncol * (nrow - 2 * TR * t)
    return pl.pallas_call(
        functools.partial(group_kernel, t),
        out_shape=jax.ShapeDtypeStruct(x.shape, F32),
        in_specs=[any_spec, pl.BlockSpec(memory_space=pltpu.VMEM), any_spec],
        out_specs=any_spec,
        scratch_shapes=[
            pltpu.VMEM((nrow, ncol), F32),
            pltpu.VMEM((2, nrow, 128), F32),
            pltpu.VMEM((2, 2, nrow, 256), BF),
            pltpu.VMEM((2, 3, 2 * TR, ncol), BF),
            pltpu.VMEM((3, 256, ncol), BF),
            pltpu.VMEM((256, ncol), F32),
            pltpu.VMEM((128, ncol), F32),
            pltpu.SemaphoreType.DMA((2, 2)),
            pltpu.SemaphoreType.DMA((2,)),
        ],
        input_output_aliases={2: 0},
        compiler_params=pltpu.CompilerParams(vmem_limit_bytes=60 * 1024 * 1024),
        cost_estimate=pl.CostEstimate(flops=flops, bytes_accessed=4 * (nrow * 128 * 8 + 2 * nrow * ncol), transcendentals=0),
        name=f"group{t}",
    )(vt, tq, x)


def solution(mesh):
    def local_apply(v_loc, t_loc, z_loc):
        num_local = t_loc.shape[0]
        t_all = lax.all_gather(t_loc, "col")
        x = z_loc
        vs = {}
        for t in range(num_local - 1, -1, -1):
            vs[t] = lax.all_gather(v_loc[TR * t:, t * 128:(t + 1) * 128], ("row", "col"))
        for t in range(num_local - 1, -1, -1):
            x = group_call(t, vs[t], t_all[:, t], x)
        return x

    return jax.shard_map(
        local_apply,
        mesh=mesh,
        in_specs=(jax.sharding.PartitionSpec("row", "col"), jax.sharding.PartitionSpec("col", None, None), jax.sharding.PartitionSpec(None, ("row", "col"))),
        out_specs=jax.sharding.PartitionSpec(None, ("row", "col")),
        check_vma=False,
    )
```

time: 3670 us -> 840 us (0.23)
  waiting for transfers between devices: 1940 us -> 326 us
  matrix products: 1470 us -> 0 us
  Pallas kernels: 0 us -> 466 us
  blocking collectives: 174 us -> 0 us
    dot_general x192 -> x0, matrix products: 1470 us -> none  [the longest x64 758 us: inner_step(): jnp.dot(v_blk, y_blk, precision=FULL_PREC, preferred_element_type=jnp.flo...]
    psum x64 -> x0, waiting for transfers between devices: 1250 us -> none  [inner_step(): w_sum = lax.psum(w_part, 'row')]
    pallas_call x0 -> x8, Pallas kernels: none -> 466 us  [group_call(): pl.pallas_call(functools.partial(group_kernel, t), out_shape=jax.ShapeDty...]
    all_gather x8 -> x9, waiting for transfers between devices: 603 us -> 326 us  [the longest x8 310 us: local_apply(): lax.all_gather(v_loc[TR * t:, t * 128:(t + 1) * 128], ('row', 'col'))]
    all_to_all x1 -> x0, blocking collectives: 95.3 us -> none  [local_apply(): return lax.all_to_all(x_two, 'row', 1, 0, tiled=True)]
    all_to_all x1 -> x0, waiting for transfers between devices: 93.9 us -> none  [local_apply(): x_two = lax.all_to_all(z_loc, 'row', 0, 1, tiled=True)]
    all_gather x8 -> x0, blocking collectives: 78.5 us -> none  [outer_step(): t_all = lax.all_gather(t_own, 'col')]
  transfers between devices with their start and end apart: 73 -> 9, of which waited for: 73 -> 9; matrix products, arithmetic and copies ran while one was open for 0% -> 3% of each run, Pallas kernels for 0% -> 44%
where the time goes in v1:
time: 840 us; the launch traced here: 837 us
  Pallas kernels  466 us (55%)
  waiting for transfers between devices  326 us (39%)
  local copies, waits for them, and re-layouts  30.5 us (4%)
  between operations  13.5 us (2%)
    pallas_call x8, Pallas kernels, group_call(): pl.pallas_call(functools.partial(group_kernel, t), out_shape=jax.ShapeDty...  466 us
    all_gather x8, waiting for transfers between devices, local_apply(): lax.all_gather(v_loc[TR * t:, t * 128:(t + 1) * 128], ('row', 'col'))  310 us
    slice x8, local copies, waits for them, and re-layouts, local_apply(): v_loc[TR * t:, t * 128:(t + 1) * 128]  19.1 us
  transfers between devices with their start and end apart: 9, of which 9 were waited for; matrix products, arithmetic and copies ran while one was open for 3% of the time, Pallas kernels for 44%

profile of v1, /device:TPU:0, one launch (start us, length us, event | category | flops | bytes accessed | tf_op | source)
XLA Modules:
  0.0 836.6 jit_solution(12769931845774263201)
XLA Ops:
  6.5 0.0 all-gather.21.cloned.1.call-start
  6.5 7.3 copy.45.x_in
  13.9 0.0 all-gather.21.cloned.1.call-update
  13.9 0.0 all-gather.35.cloned.1.call-start
  13.9 1.7 slice.62
  15.6 0.0 all-gather.35.cloned.1.call-update
  15.6 0.0 all-gather.33.cloned.1.call-start
  15.7 1.9 slice.60
  17.6 0.0 all-gather.33.cloned.1.call-update
  17.6 0.0 all-gather.31.cloned.1.call-start
  17.6 2.1 slice.58
  19.7 0.0 all-gather.31.cloned.1.call-update
  19.8 0.0 all-gather.29.cloned.1.call-start
  19.8 2.3 slice.56
  22.1 0.0 all-gather.29.cloned.1.call-update
  22.1 0.0 all-gather.27.cloned.1.call-start
  22.2 2.5 slice.54
  24.6 0.0 all-gather.27.cloned.1.call-update
  24.7 0.0 all-gather.25.cloned.1.call-start
  24.7 2.7 slice.52
  27.4 0.0 all-gather.25.cloned.1.call-update
  27.4 0.0 all-gather.23.cloned.1.call-start
  27.5 2.9 slice.50
  30.4 0.0 all-gather.23.cloned.1.call-update
  30.4 0.0 all-gather.19.cloned.1.call-start
  30.4 3.1 slice.48
  33.5 0.0 all-gather.19.cloned.1.call-update
  33.5 15.9 %all-gather.21.cloned.1.call-done = f32[64,128,128]{2,1,0:T(8,128)} async-done(((f32[8,128,128]{2,1,0:T(8,128)}), f32[64,128,128]{2,1,0:T(8,128)}) %all-gather.21.cloned.1.call-update) | async-done | bytes 4194320 | tf_op jit(solution)/shard_map/all_gather | solution.py:162
  49.4 4.1 slice_bitcast_fusion
  53.5 33.2 %all-gather.35.cloned.1.call-done = f32[8192,128]{1,0:T(8,128)} async-done(((f32[512,128]{1,0:T(8,128)}), f32[8192,128]{1,0:T(8,128)}) %all-gather.35.cloned.1.call-update) | async-done | bytes 4194320 | tf_op jit(solution)/shard_map/all_gather | solution.py:166
  86.7 18.2 %group7.1.x_in = f32[8192,256]{1,0:T(8,128)} custom-call(f32[16,512,128]{2,1,0:T(8,128)} %bitcast.49, f32[8,128,128]{2,1,0:T(8,128)} %get-tuple-element.5.tq, f32[8192,256]{1,0:T(8,128)} %copy.45.x_in), custom_call_target="tpu_custom_call", output_to_operand_aliasing={{}: (2, {})} | custom-call | flops 6442450944 | bytes 50331648 | tf_op jit(solution)/shard_map/group7/pallas_call | solution.py:136
  104.9 32.8 %all-gather.33.cloned.1.call-done = f32[16384,128]{1,0:T(8,128)} async-done(((f32[1024,128]{1,0:T(8,128)}), f32[16384,128]{1,0:T(8,128)}) %all-gather.33.cloned.1.call-update) | async-done | bytes 8388624 | tf_op jit(solution)/shard_map/all_gather | solution.py:166
  137.6 27.3 %group6.1.x_in = f32[8192,256]{1,0:T(8,128)} custom-call(f32[16,1024,128]{2,1,0:T(8,128)} %bitcast.48, f32[8,128,128]{2,1,0:T(8,128)} %get-tuple-element.6.tq, f32[8192,256]{1,0:T(8,128)} %group7.1.x_in), custom_call_target="tpu_custom_call", output_to_operand_aliasing={{}: (2, {})} | custom-call | flops 12884901888 | bytes 50331648 | tf_op jit(solution)/shard_map/group6/pallas_call | solution.py:136
  165.0 37.1 %all-gather.31.cloned.1.call-done = f32[24576,128]{1,0:T(8,128)} async-done(((f32[1536,128]{1,0:T(8,128)}), f32[24576,128]{1,0:T(8,128)}) %all-gather.31.cloned.1.call-update) | async-done | bytes 12582928 | tf_op jit(solution)/shard_map/all_gather | solution.py:166
  202.1 41.4 %group5.1.x_in = f32[8192,256]{1,0:T(8,128)} custom-call(f32[16,1536,128]{2,1,0:T(8,128)} %bitcast.47, f32[8,128,128]{2,1,0:T(8,128)} %get-tuple-element.7.tq, f32[8192,256]{1,0:T(8,128)} %group6.1.x_in), custom_call_target="tpu_custom_call", output_to_operand_aliasing={{}: (2, {})} | custom-call | flops 19327352832 | bytes 50331648 | tf_op jit(solution)/shard_map/group5/pallas_call | solution.py:136
  243.5 36.8 %all-gather.29.cloned.1.call-done = f32[32768,128]{1,0:T(8,128)} async-done(((f32[2048,128]{1,0:T(8,128)}), f32[32768,128]{1,0:T(8,128)}) %all-gather.29.cloned.1.call-update) | async-done | bytes 16777232 | tf_op jit(solution)/shard_map/all_gather | solution.py:166
  280.3 53.0 %group4.1.x_in = f32[8192,256]{1,0:T(8,128)} custom-call(f32[16,2048,128]{2,1,0:T(8,128)} %bitcast.46, f32[8,128,128]{2,1,0:T(8,128)} %get-tuple-element.8.tq, f32[8192,256]{1,0:T(8,128)} %group5.1.x_in), custom_call_target="tpu_custom_call", output_to_operand_aliasing={{}: (2, {})} | custom-call | flops 25769803776 | bytes 50331648 | tf_op jit(solution)/shard_map/group4/pallas_call | solution.py:136
  333.3 38.8 %all-gather.27.cloned.1.call-done = f32[40960,128]{1,0:T(8,128)} async-done(((f32[2560,128]{1,0:T(8,128)}), f32[40960,128]{1,0:T(8,128)}) %all-gather.27.cloned.1.call-update) | async-done | bytes 20971536 | tf_op jit(solution)/shard_map/all_gather | solution.py:166
  372.1 64.2 %group3.1.x_in = f32[8192,256]{1,0:T(8,128)} custom-call(f32[16,2560,128]{2,1,0:T(8,128)} %bitcast.45, f32[8,128,128]{2,1,0:T(8,128)} %get-tuple-element.9.tq, f32[8192,256]{1,0:T(8,128)} %group4.1.x_in), custom_call_target="tpu_custom_call", output_to_operand_aliasing={{}: (2, {})} | custom-call | flops 32212254720 | bytes 50331648 | tf_op jit(solution)/shard_map/group3/pallas_call | solution.py:136
  436.4 41.4 %all-gather.25.cloned.1.call-done = f32[49152,128]{1,0:T(8,128)} async-done(((f32[3072,128]{1,0:T(8,128)}), f32[49152,128]{1,0:T(8,128)}) %all-gather.25.cloned.1.call-update) | async-done | bytes 25165840 | tf_op jit(solution)/shard_map/all_gather | solution.py:166
  477.8 76.0 %group2.1.x_in = f32[8192,256]{1,0:T(8,128)} custom-call(f32[16,3072,128]{2,1,0:T(8,128)} %bitcast.44, f32[8,128,128]{2,1,0:T(8,128)} %get-tuple-element.10.tq, f32[8192,256]{1,0:T(8,128)} %group3.1.x_in), custom_call_target="tpu_custom_call", output_to_operand_aliasing={{}: (2, {})} | custom-call | flops 38654705664 | bytes 50331648 | tf_op jit(solution)/shard_map/group2/pallas_call | solution.py:136
  553.8 43.8 %all-gather.23.cloned.1.call-done = f32[57344,128]{1,0:T(8,128)} async-done(((f32[3584,128]{1,0:T(8,128)}), f32[57344,128]{1,0:T(8,128)}) %all-gather.23.cloned.1.call-update) | async-done | bytes 29360144 | tf_op jit(solution)/shard_map/all_gather | solution.py:166
  597.6 87.1 %group1.1.x_in = f32[8192,256]{1,0:T(8,128)} custom-call(f32[16,3584,128]{2,1,0:T(8,128)} %bitcast.43, f32[8,128,128]{2,1,0:T(8,128)} %get-tuple-element.11.tq, f32[8192,256]{1,0:T(8,128)} %group2.1.x_in), custom_call_target="tpu_custom_call", output_to_operand_aliasing={{}: (2, {})} | custom-call | flops 45097156608 | bytes 50331648 | tf_op jit(solution)/shard_map/group1/pallas_call | solution.py:136
  684.7 46.6 %all-gather.19.cloned.1.call-done = f32[65536,128]{1,0:T(8,128)} async-done(((f32[4096,128]{1,0:T(8,128)}), f32[65536,128]{1,0:T(8,128)}) %all-gather.19.cloned.1.call-update) | async-done | bytes 33554448 | tf_op jit(solution)/shard_map/all_gather | solution.py:166
  731.3 98.5 %group0.1 = f32[8192,256]{1,0:T(8,128)} custom-call(f32[16,4096,128]{2,1,0:T(8,128)} %bitcast.42, f32[8,128,128]{2,1,0:T(8,128)} %get-tuple-element.12.tq, f32[8192,256]{1,0:T(8,128)} %group1.1.x_in), custom_call_target="tpu_custom_call", output_to_operand_aliasing={{}: (2, {})} | custom-call | flops 51539607552 | bytes 50331648 | tf_op jit(solution)/shard_map/group0/pallas_call | solution.py:136
Async XLA Ops:
  6.5 42.9 %all-gather.21.cloned.1.call-start = ((), (), s32[]{:S(2)}) async-start(), calls=%async_computation.1 | async-start | bytes 4718592 | tf_op jit(solution)/shard_map/all_gather | solution.py:162
  13.9 72.8 %all-gather.35.cloned.1.call-start = ((), (), s32[]{:S(2)}) async-start(), calls=%async_computation.8 | async-start | bytes 4456448 | tf_op jit(solution)/shard_map/all_gather | solution.py:166
  15.6 122.0 %all-gather.33.cloned.1.call-start = ((), (), s32[]{:S(2)}) async-start(), calls=%async_computation.7 | async-start | bytes 8912896 | tf_op jit(solution)/shard_map/all_gather | solution.py:166
  17.6 184.5 %all-gather.31.cloned.1.call-start = ((), (), s32[]{:S(2)}) async-start(), calls=%async_computation.6 | async-start | bytes 13369344 | tf_op jit(solution)/shard_map/all_gather | solution.py:166
  19.8 260.5 %all-gather.29.cloned.1.call-start = ((), (), s32[]{:S(2)}) async-start(), calls=%async_computation.5 | async-start | bytes 17825792 | tf_op jit(solution)/shard_map/all_gather | solution.py:166
  22.1 350.0 %all-gather.27.cloned.1.call-start = ((), (), s32[]{:S(2)}) async-start(), calls=%async_computation.4 | async-start | bytes 22282240 | tf_op jit(solution)/shard_map/all_gather | solution.py:166
  24.7 453.1 %all-gather.25.cloned.1.call-start = ((), (), s32[]{:S(2)}) async-start(), calls=%async_computation.3 | async-start | bytes 26738688 | tf_op jit(solution)/shard_map/all_gather | solution.py:166
  27.4 570.2 %all-gather.23.cloned.1.call-start = ((), (), s32[]{:S(2)}) async-start(), calls=%async_computation.2 | async-start | bytes 31195136 | tf_op jit(solution)/shard_map/all_gather | solution.py:166
  30.4 700.9 %all-gather.19.cloned.1.call-start = ((), (), s32[]{:S(2)}) async-start(), calls=%async_computation | async-start | bytes 35651584 | tf_op jit(solution)/shard_map/all_gather | solution.py:166
Sparse Core Ops, SparseCore 0:
  14.0 35.3 all-gather.20
  51.7 35.0 all-gather.34
  89.0 48.6 all-gather.32
  139.7 62.3 all-gather.30
  204.2 76.0 all-gather.28
  282.3 89.7 all-gather.26
  374.4 103.3 all-gather.24
  480.0 117.5 all-gather.22
  599.9 131.3 all-gather.18

commit v2 on v0

v2 whole, which is shorter than its diff:
```python
import jax
import jax.numpy as jnp
from jax import lax
from jax.experimental import pallas as pl
from jax.experimental.pallas import tpu as pltpu
from jax.sharding import PartitionSpec as P

BF = jnp.bfloat16
F32 = jnp.float32
TN = (((0,), (0,)), ((), ()))
TR = 512
BW = 128
NT = 8
NPAIR = 4 * NT
NSLOT = 2 * NT * (NT + 1)
MESH = pl.DeviceIdType.MESH
HOP_LAG = 12
DONE_LAG = 52


def split3(v):
    h = v.astype(BF)
    r = v - h.astype(F32)
    m = r.astype(BF)
    l = (r - m.astype(F32)).astype(BF)
    return h, m, l


def mm(a, b):
    return jnp.dot(a, b, preferred_element_type=F32)


def mmt(a, b):
    return lax.dot_general(a, b, TN, preferred_element_type=F32)


def stage1(half, off, p, X, VF, C, XS, YC, wacc, src, dst):
    for r in range(2):
        rows = pl.ds(pl.multiple_of(r * half + off, TR), TR)
        x = X[rows, :]
        x = x - (mm(C[src, 0, rows, :], YC[0]) + mm(C[src, 0, rows, :], YC[1]) + mm(C[src, 1, rows, :], YC[2]))
        X[rows, :] = x
        if wacc:
            prow = pl.ds(r * TR, TR)
            xh, xm, xl = split3(x)
            XS[p, 0, prow, :] = xh
            XS[p, 1, prow, :] = xm
            XS[p, 2, prow, :] = xl
            vh, vm, vl = split3(VF[dst, rows, :])
            C[dst, 0, rows, :BW] = vh
            C[dst, 0, rows, BW:] = vm
            C[dst, 1, rows, :BW] = vh
            C[dst, 1, rows, BW:] = vl


def stage2(half, off, p, C, XS, A, B, dst):
    a = A[...]
    b = B[...]
    for r in range(2):
        rows = pl.ds(pl.multiple_of(r * half + off, TR), TR)
        prow = pl.ds(r * TR, TR)
        n1 = C[dst, 0, rows, :]
        a += mmt(n1, XS[p, 0, prow, :]) + mmt(n1, XS[p, 1, prow, :])
        b += mmt(C[dst, 1, rows, BW:], XS[p, 0, prow, :]) + mmt(n1[:, :BW], XS[p, 2, prow, :])
    A[...] = a
    B[...] = b


def make_y(tq, A, B, YC):
    w = A[:BW, :] + A[BW:, :] + B[...]
    th, tm, tl = split3(tq)
    wh, wm, wl = split3(w)
    t1 = jnp.concatenate([th, tm], axis=1)
    t2 = jnp.concatenate([th, tl], axis=1)
    y = (
        mm(t1, jnp.concatenate([wh, wh], axis=0))
        + mm(t1, jnp.concatenate([wm, wm], axis=0))
        + mm(t2, jnp.concatenate([wl, wh], axis=0))
    )
    yh, ym, yl = split3(y)
    YC[0] = jnp.concatenate([yh, yh], axis=0)
    YC[1] = jnp.concatenate([ym, ym], axis=0)
    YC[2] = jnp.concatenate([yl, yh], axis=0)
    A[...] = jnp.zeros_like(A)
    B[...] = jnp.zeros_like(B)


def kernel(v_loc, head, x_in, x_out, G, X, VF, C, XS, YC, A, B, TQ, recv, sib, vsem, xsem, send):
    half = X.shape[0] // 2
    z0 = lax.axis_index("row")
    c0 = lax.axis_index("col")
    y0 = c0 // 4
    x0 = (c0 // 2) % 2
    k0 = c0 % 2
    me = (x0, y0, z0)
    partner = (z0, c0 + 1 - 2 * k0)
    peers = ((z0, c0 + 2 - 4 * x0), (z0, c0 + 4 - 8 * y0), (1 - z0, c0))

    def pair_of(pr):
        w = pr // 4 + 1
        return w, NT - w, 3 - pr % 4

    def decode(s):
        w = 1
        for v in range(1, NT):
            w = w + (s >= 2 * v * (v + 1)).astype(jnp.int32)
        rem = s - 2 * w * (w - 1)
        back = (rem >= w).astype(jnp.int32) + (rem >= 2 * w).astype(jnp.int32) + (rem >= 3 * w).astype(jnp.int32)
        return w, 3 - back, rem - back * w

    def slot_of(w, p, i):
        return 2 * w * (w - 1) + (3 - p) * w + i

    def xcopy_in():
        return pltpu.make_async_copy(x_in, X, xsem.at[0, 0])

    xcopy_in().start()
    barrier = pltpu.get_barrier_semaphore()
    for dev in (*peers, partner):
        pl.semaphore_signal(barrier, inc=1, device_id=dev, device_id_type=MESH)
    pl.semaphore_wait(barrier, 4)

    def push(src, s, r, dev, sem_arr, which):
        pltpu.make_async_remote_copy(
            src_ref=src,
            dst_ref=G.at[s, k0, r],
            send_sem=send.at[which],
            recv_sem=sem_arr.at[s, r],
            device_id=dev,
            device_id_type=MESH,
        ).start()

    rows3 = (z0, z0, 1 - z0)
    cols3 = (c0 + 2 - 4 * x0, c0 + 4 - 8 * y0, c0)

    def turn(k, v, j):
        a, b, c = v[j % 3], v[(j + 1) % 3], v[(j + 2) % 3]
        return jnp.where(k == 0, a, jnp.where(k == 1, b, c))

    def chunk(t, i):
        rows = pl.ds(pl.multiple_of((t + i) * TR, TR), TR)
        return v_loc.at[rows, pl.ds(pl.multiple_of(t * BW, BW), BW)]

    def hop(s, depth):
        w, p, i = decode(s)
        k = (i + w) % 3
        xy = ((x0 + p) % 2, (y0 + p // 2) % 2)
        for r in range(2):
            bits = (xy[0], xy[1], (z0 + r) % 2)
            e0, e1, e2 = turn(k, bits, 0), turn(k, bits, 1), turn(k, bits, 2)
            far = e1 + e2
            mine = jnp.where(e0 + far == 0, 0, 2 - e0 + far)

            @pl.when(mine == depth)
            def _():
                to = [(turn(k, rows3, j), turn(k, cols3, j)) for j in range(3)]

                @pl.when(mine == 0)
                def _():
                    @pl.when(i == 0)
                    def _():
                        o = head.at[w - 1]
                        push(o, s, r, to[0], recv, 0)
                        push(o, s, r, partner, sib, 1)

                    @pl.when(i > 0)
                    def _():
                        o = chunk(NT - w, i)
                        push(o, s, r, to[0], recv, 0)
                        push(o, s, r, partner, sib, 1)

                @pl.when(mine > 0)
                def _():
                    g = G.at[s, k0, r]
                    pltpu.make_async_copy(g, g, recv.at[s, r]).wait()

                    @pl.when(e0 == 1)
                    def _():
                        @pl.when(far == 0)
                        def _():
                            push(g, s, r, to[1], recv, 0)

                        @pl.when(e2 == 0)
                        def _():
                            push(g, s, r, to[2], recv, 0)

                        @pl.when(far > 0)
                        def _():
                            push(g, s, r, to[0], recv, 0)

                    push(g, s, r, partner, sib, 1)

    def tick(tau):
        def one(h, carry):
            s = tau - jnp.where(h == 0, 0, 1 + HOP_LAG * h)

            @pl.when(jnp.logical_and(s >= 0, s < NSLOT))
            def _():
                hop(s, h)

            return carry

        lax.fori_loop(0, 5, one, 0)

    def ticks(lo, hi):
        def one(tau, carry):
            tick(tau)
            return carry

        lax.fori_loop(lo, hi, one, 0)

    def start_of(n):
        w, t, p = pair_of(n // 2)
        return slot_of(w, p, 0) + w + DONE_LAG + (n % 2) * (w // 2)

    def await_sibling(pr):
        w, t, p = pair_of(pr)

        def one(i, carry):
            for r in range(2):
                g = G.at[slot_of(w, p, i), 1 - k0, r]
                pltpu.make_async_copy(g, g, sib.at[slot_of(w, p, i), r]).wait()
            return carry

        lax.fori_loop(0, w, one, 0)

    def load(n, slot, wait):
        pr = n // 2
        b = 1 - n % 2
        w, t, p = pair_of(pr)

        def one(i, carry):
            for r in range(2):
                dst = VF.at[slot, pl.ds(pl.multiple_of(r * half + (t + i) * TR, TR), TR), :]
                if wait:
                    pltpu.make_async_copy(G.at[0, 0, 0], dst, vsem.at[slot, i, r]).wait()
                else:
                    is_own = jnp.logical_and(jnp.logical_and(z0 == r, b == k0), c0 // 2 == p)

                    @pl.when(jnp.logical_and(is_own, i == 0))
                    def _():
                        pltpu.make_async_copy(head.at[w - 1], dst, vsem.at[slot, i, r]).start()

                    @pl.when(jnp.logical_and(is_own, i > 0))
                    def _():
                        pltpu.make_async_copy(chunk(t, i), dst, vsem.at[slot, i, r]).start()

                    @pl.when(jnp.logical_not(is_own))
                    def _():
                        pltpu.make_async_copy(G.at[slot_of(w, p, i), b, r], dst, vsem.at[slot, i, r]).start()
            return carry

        lax.fori_loop(0, w, one, 0)

    def compute(n):
        pr = n // 2
        b = 1 - n % 2
        dst = n % 2
        src = 1 - dst
        w, t, p = pair_of(pr)
        first = t * TR

        @pl.when(n % 8 == 0)
        def _():
            for r in range(2):
                rows = pl.ds(pl.multiple_of(r * half + first, TR), TR)
                C[src, :, rows, :] = jnp.zeros((2, TR, 2 * BW), BF)

        drow = pl.ds(pl.multiple_of(b * half + first + BW * p, BW), BW)
        blk = VF[dst, drow, :]
        ri = lax.broadcasted_iota(jnp.int32, (BW, BW), 0)
        ci = lax.broadcasted_iota(jnp.int32, (BW, BW), 1)
        TQ[...] = jnp.where(ci >= ri, blk, 0.0)
        VF[dst, drow, :] = jnp.where(ri > ci, blk, jnp.where(ri == ci, 1.0, 0.0))

        stage1(half, first, 0, X, VF, C, XS, YC, True, src, dst)
        now = start_of(n)

        def body(i, carry):
            q = lax.rem(i, 2)
            stage2(half, first + (i - 1) * TR, 1 - q, C, XS, A, B, dst)
            stage1(half, first + i * TR, q, X, VF, C, XS, YC, True, src, dst)

            @pl.when(q == 1)
            def _():
                tick(now + i // 2)

            return carry

        lax.fori_loop(1, w, body, 0)

        @pl.when(n < 2 * NPAIR - 1)
        def _():
            ticks(now + w // 2, start_of(n + 1))

            @pl.when(n % 2 == 1)
            def _():
                await_sibling(pr + 1)

            load(n + 1, src, False)

        stage2(half, first + (w - 1) * TR, lax.rem(w - 1, 2), C, XS, A, B, dst)
        make_y(TQ[...], A, B, YC)

    A[...] = jnp.zeros_like(A)
    B[...] = jnp.zeros_like(B)
    YC[...] = jnp.zeros_like(YC)

    ticks(0, start_of(0))
    await_sibling(0)
    load(0, 0, False)
    xcopy_in().wait()

    def panel(n, carry):
        load(n, n % 2, True)
        compute(n)
        return carry

    lax.fori_loop(0, 2 * NPAIR, panel, 0)

    def xcopy_out(i, r):
        rows = pl.ds(pl.multiple_of(r * half + i * TR, TR), TR)
        return pltpu.make_async_copy(X.at[rows, :], x_out.at[rows, :], xsem.at[i, r])

    def finish(i, carry):
        stage1(half, i * TR, 0, X, VF, C, XS, YC, False, 1, 0)
        for r in range(2):
            xcopy_out(i, r).start()
        return carry

    lax.fori_loop(0, NT, finish, 0)

    def drain(i, carry):
        for r in range(2):
            xcopy_out(i, r).wait()
        return carry

    lax.fori_loop(0, NT, drain, 0)
    nown = NT * (NT + 1) // 2
    sent = G.at[pl.ds(0, 7 * nown // 4)]
    pltpu.make_async_copy(sent, sent, send.at[0]).wait()
    given = G.at[pl.ds(0, 8 * nown // 4)]
    pltpu.make_async_copy(given, given, send.at[1]).wait()


def pack_heads(v_loc, t_loc):
    r = lax.axis_index("row")
    q = lax.axis_index("col")
    off = BW * ((q - r) // 2)
    has = q % 2 == r
    ri = lax.broadcasted_iota(jnp.int32, (NT, TR, BW), 1) - off
    ci = lax.broadcasted_iota(jnp.int32, (NT, TR, BW), 2)
    mask = has & (ri >= 0) & (ri < BW) & (ci >= ri)
    heads = jnp.stack([v_loc[t * TR : (t + 1) * TR, t * BW : (t + 1) * BW] for t in range(NT - 1, -1, -1)])
    t_pad = jnp.pad(t_loc[::-1], ((0, 0), (TR, TR - BW), (0, 0)))
    return jnp.where(mask, lax.dynamic_slice_in_dim(t_pad, TR - off, TR, axis=1), heads)


def solution(mesh):
    def local_apply(v_loc, t_loc, z_loc):
        nrow, ncol = z_loc.shape
        head = pack_heads(v_loc, t_loc)
        any_spec = pl.BlockSpec(memory_space=pl.ANY)
        x, _ = pl.pallas_call(
            kernel,
            out_shape=(
                jax.ShapeDtypeStruct((nrow, ncol), F32),
                jax.ShapeDtypeStruct((NSLOT, 2, 2, TR, BW), F32),
            ),
            in_specs=[any_spec, any_spec, any_spec],
            out_specs=(any_spec, any_spec),
            scratch_shapes=[
                pltpu.VMEM((nrow, ncol), F32),
                pltpu.VMEM((2, nrow, BW), F32),
                pltpu.VMEM((2, 2, nrow, 2 * BW), BF),
                pltpu.VMEM((2, 3, 2 * TR, ncol), BF),
                pltpu.VMEM((3, 2 * BW, ncol), BF),
                pltpu.VMEM((2 * BW, ncol), F32),
                pltpu.VMEM((BW, ncol), F32),
                pltpu.VMEM((BW, BW), F32),
                pltpu.SemaphoreType.DMA((NSLOT, 2)),
                pltpu.SemaphoreType.DMA((NSLOT, 2)),
                pltpu.SemaphoreType.DMA((2, NT, 2)),
                pltpu.SemaphoreType.DMA((NT, 2)),
                pltpu.SemaphoreType.DMA((2,)),
            ],
            compiler_params=pltpu.CompilerParams(
                collective_id=0, has_side_effects=True, vmem_limit_bytes=60 * 1024 * 1024
            ),
            name="back_transform",
        )(v_loc, head, z_loc)
        return x

    return jax.shard_map(
        local_apply,
        mesh=mesh,
        in_specs=(P("row", "col"), P("col", None, None), P(None, ("row", "col"))),
        out_specs=P(None, ("row", "col")),
        check_vma=False,
    )
```

time: 3670 us -> 636 us (0.17)
  waiting for transfers between devices: 1940 us -> 0 us
  matrix products: 1470 us -> 0 us
  Pallas kernels: 0 us -> 616 us
  blocking collectives: 174 us -> 0 us
  local copies, waits for them, and re-layouts: 56.4 us -> 16.2 us
    dot_general x192 -> x0, matrix products: 1470 us -> none  [the longest x64 758 us: inner_step(): jnp.dot(v_blk, y_blk, precision=FULL_PREC, preferred_element_type=jnp.flo...]
    psum x64 -> x0, waiting for transfers between devices: 1250 us -> none  [inner_step(): w_sum = lax.psum(w_part, 'row')]
    pallas_call x0 -> x1, Pallas kernels: none -> 616 us  [local_apply(): pl.pallas_call(kernel, out_shape=(jax.ShapeDtypeStruct((nrow, ncol), F32)...]
    all_gather x8 -> x0, waiting for transfers between devices: 603 us -> none  [outer_step(): v_all = lax.all_gather(v_own, 'col')]
    all_to_all x1 -> x0, blocking collectives: 95.3 us -> none  [local_apply(): return lax.all_to_all(x_two, 'row', 1, 0, tiled=True)]
    all_to_all x1 -> x0, waiting for transfers between devices: 93.9 us -> none  [local_apply(): x_two = lax.all_to_all(z_loc, 'row', 0, 1, tiled=True)]
    all_gather x8 -> x0, blocking collectives: 78.5 us -> none  [outer_step(): t_all = lax.all_gather(t_own, 'col')]
  transfers between devices with their start and end apart: 73 -> 0, of which waited for: 73 -> 0; matrix products, arithmetic and copies ran while one was open for 0% -> 0% of each run, Pallas kernels for 0% -> 0%
where the time goes in v2:
time: 636 us; the launch traced here: 634 us
  Pallas kernels  616 us (97%)
  local copies, waits for them, and re-layouts  16.2 us (3%)
    pallas_call x1, Pallas kernels, local_apply(): pl.pallas_call(kernel, out_shape=(jax.ShapeDtypeStruct((nrow, ncol), F32)...  616 us
    unnamed x8, local copies, waits for them, and re-layouts  14.1 us

profile of v2, /device:TPU:0, one launch (start us, length us, event | category | flops | bytes accessed | tf_op | source)
XLA Modules:
  0.0 634.1 jit_solution(385644301554242774)
XLA Ops:
  0.0 1.1 rev.3
  1.1 1.0 bitcast_dynamic-update-slice_fusion.7
  2.1 1.0 bitcast_dynamic-update-slice_fusion.6
  3.0 1.0 bitcast_dynamic-update-slice_fusion.5
  4.0 1.0 bitcast_dynamic-update-slice_fusion.4
  5.0 1.0 bitcast_dynamic-update-slice_fusion.3
  6.0 1.0 bitcast_dynamic-update-slice_fusion.2
  6.9 1.0 bitcast_dynamic-update-slice_fusion.1
  7.9 1.0 bitcast_dynamic-update-slice_fusion
  8.9 1.7 fusion.head
  10.6 616.2 %back_transform.1 = (f32[8192,256]{1,0:T(8,128)}, f32[144,2,2,512,128]{4,3,2,1,0:T(8,128)}) custom-call(f32[4096,1024]{1,0:T(8,128)} %v_loc.1, f32[8,512,128]{2,1,0:T(8,128)} %fusion.head, f32[8192,256]{1,0:T(8,128)} %x_in.1), custom_call_target="tpu_custom_call" | custom-call | tf_op jit(solution)/shard_map/back_transform/pallas_call | solution.py:364
  626.8 7.3 %copy.12 = f32[8192,256]{1,0:T(8,128)} copy(f32[8192,256]{1,0:T(8,128)} %get-tuple-element.6) | data formatting | bytes 16777216
  (2 shorter events, 0.0 us)

commit v3 on v2

--- a/solution.py
+++ b/solution.py
@@ -14,8 +14,7 @@
 NPAIR = 4 * NT
 NSLOT = 2 * NT * (NT + 1)
 MESH = pl.DeviceIdType.MESH
-HOP_LAG = 12
-DONE_LAG = 52
+LAGS = ((3, 4), (5, 7), (NT, 10))
 
 
 def split3(v):
@@ -192,7 +191,13 @@
 
     def tick(tau):
         def one(h, carry):
-            s = tau - jnp.where(h == 0, 0, 1 + HOP_LAG * h)
+            s = jnp.int32(-1)
+            for j, (top, lag) in enumerate(LAGS):
+                bottom = LAGS[j - 1][0] if j else 0
+                cand = tau - 1 - lag * h
+                fits = jnp.logical_and(cand >= 2 * bottom * (bottom + 1), cand < 2 * top * (top + 1))
+                s = jnp.where(fits, cand, s)
+            s = jnp.where(h == 0, tau, s)
 
             @pl.when(jnp.logical_and(s >= 0, s < NSLOT))
             def _():
@@ -211,7 +216,10 @@
 
     def start_of(n):
         w, t, p = pair_of(n // 2)
-        return slot_of(w, p, 0) + w + DONE_LAG + (n % 2) * (w // 2)
+        done = jnp.int32(0)
+        for top, lag in LAGS[::-1]:
+            done = jnp.where(w <= top, 4 * lag + 4, done)
+        return slot_of(w, p, 0) + w + done + (n % 2) * (w // 2)
 
     def await_sibling(pr):
         w, t, p = pair_of(pr)

time: 636 us -> 700 us (1.10)
  Pallas kernels: 616 us -> 680 us
    pallas_call x1, Pallas kernels: 616 us -> 680 us  [local_apply(): pl.pallas_call(kernel, out_shape=(jax.ShapeDtypeStruct((nrow, ncol), F32)...]
where the time goes in v3:
time: 700 us; the launch traced here: 698 us
  Pallas kernels  680 us (97%)
  local copies, waits for them, and re-layouts  16.2 us (2%)
    pallas_call x1, Pallas kernels, local_apply(): pl.pallas_call(kernel, out_shape=(jax.ShapeDtypeStruct((nrow, ncol), F32)...  680 us
    unnamed x8, local copies, waits for them, and re-layouts  14.1 us

profile of v3, /device:TPU:0, one launch (start us, length us, event | category | flops | bytes accessed | tf_op | source)
XLA Modules:
  0.0 698.2 jit_solution(7502588409632495401)
XLA Ops:
  0.0 1.1 rev.3
  1.1 1.0 bitcast_dynamic-update-slice_fusion.7
  2.1 1.0 bitcast_dynamic-update-slice_fusion.6
  3.0 1.0 bitcast_dynamic-update-slice_fusion.5
  4.0 1.0 bitcast_dynamic-update-slice_fusion.4
  5.0 1.0 bitcast_dynamic-update-slice_fusion.3
  6.0 1.0 bitcast_dynamic-update-slice_fusion.2
  6.9 1.0 bitcast_dynamic-update-slice_fusion.1
  7.9 1.0 bitcast_dynamic-update-slice_fusion
  8.9 1.7 fusion.head
  10.6 680.3 %back_transform.1 = (f32[8192,256]{1,0:T(8,128)}, f32[144,2,2,512,128]{4,3,2,1,0:T(8,128)}) custom-call(f32[4096,1024]{1,0:T(8,128)} %v_loc.1, f32[8,512,128]{2,1,0:T(8,128)} %fusion.head, f32[8192,256]{1,0:T(8,128)} %x_in.1), custom_call_target="tpu_custom_call" | custom-call | tf_op jit(solution)/shard_map/back_transform/pallas_call | solution.py:372
  690.8 7.3 %copy.12 = f32[8192,256]{1,0:T(8,128)} copy(f32[8192,256]{1,0:T(8,128)} %get-tuple-element.6) | data formatting | bytes 16777216
  (2 shorter events, 0.0 us)
